TPU v7x, 32 devices: a 4x4x1 block of a 4x4x8 slice. The times are simulated.
32 devices in a mesh: dp: 1 (over z), ing: 4 (over y), grp: 8 (over x, core).
Axes of the slice: x: 4, y: 4, z: 1, core: 2. Of those that a mesh axis runs over, the one named last changes fastest.
The devices are a block of a 4x4x8 slice.
Arguments:
- x_first: bfloat16 [49152, 1024], P(('dp', 'grp', 'ing'))
- ids_first: int32 [49152, 8], P(('dp', 'grp', 'ing'))
- gates_first: float32 [49152, 8], P(('dp', 'grp', 'ing'))
- x_second: bfloat16 [49152, 1024], P(('dp', 'grp', 'ing'))
- ids_second: int32 [49152, 8], P(('dp', 'grp', 'ing'))
- gates_second: float32 [49152, 8], P(('dp', 'grp', 'ing'))
- w_one: bfloat16 [32, 1024, 512], P(('grp', 'ing'))
- w_three: bfloat16 [32, 1024, 512], P(('grp', 'ing'))
- w_two: bfloat16 [32, 512, 1024], P(('grp', 'ing'))
Outputs:
- output 1: bfloat16 [49152, 1024], P(('dp', 'grp', 'ing'))
- output 2: bfloat16 [49152, 1024], P(('dp', 'grp', 'ing'))
All inputs are finite; a program needn't handle non-finite values.
Results may differ from a plain program's by a relative error of at most 0.0087765.
Values are sent between devices in bfloat16 or wider.
A program may use at most 768 MiB of HBM per device.

v0:
```python
import jax
import jax.numpy as jnp
from jax import lax
from jax.sharding import PartitionSpec as P


def solution(mesh):
    n_grp = mesh.shape['grp']
    n_ing = mesh.shape['ing']
    tok_spec = P(('dp', 'grp', 'ing'), None)
    w_spec = P(('grp', 'ing'), None, None)

    def moe_local(x_loc, ids_loc, gates_loc, w_one, w_three, w_two):
        tokens, hidden = x_loc.shape
        top_k = ids_loc.shape[1]
        local_e = w_one.shape[0]
        per_group = local_e * n_ing
        experts = per_group * n_grp
        limit_m = min(top_k, n_grp // 2)
        cap_group = tokens * limit_m // n_grp
        cap_expert = limit_m * (-(-(tokens * (top_k // limit_m)) // experts))

        expert_hit = ids_loc[:, :, None] == jnp.arange(experts)
        gate_full = jnp.sum(jnp.where(expert_hit, gates_loc[:, :, None], 0.0), axis=1).reshape(tokens, n_grp, per_group)
        grp_member = jnp.any(expert_hit.reshape(tokens, top_k, n_grp, per_group), axis=(1, 3))
        grp_slot = jnp.cumsum(grp_member.astype(jnp.int32), axis=0) - 1
        send_sel = grp_member.T[:, None, :] & (grp_slot.T[:, None, :] == jnp.arange(cap_group)[:, None])
        send_bf = send_sel.astype(jnp.bfloat16)
        send_x = jnp.einsum('hsu,ue->hse', send_bf, x_loc, preferred_element_type=jnp.float32).astype(jnp.bfloat16)
        send_gate = jnp.einsum('hsu,uhf->hsf', send_sel.astype(jnp.float32), gate_full, precision=lax.Precision.HIGHEST)
        recv_x = lax.all_to_all(send_x, 'grp', 0, 0, tiled=True)
        recv_gate = lax.all_to_all(send_gate, 'grp', 0, 0, tiled=True)

        member = recv_gate > 0.0
        exp_slot = jnp.cumsum(member.astype(jnp.int32), axis=1) - 1
        mem_er = jnp.swapaxes(member, 1, 2)[:, :, None, :]
        slot_er = jnp.swapaxes(exp_slot, 1, 2)[:, :, None, :]
        disp_sel = mem_er & (slot_er == jnp.arange(cap_expert)[:, None])
        disp_bf = disp_sel.astype(jnp.bfloat16)
        slot_gate = jnp.sum(jnp.where(disp_sel, jnp.swapaxes(recv_gate, 1, 2)[:, :, None, :], 0.0), axis=-1)
        expert_in = jnp.einsum('secr,srd->escd', disp_bf, recv_x, preferred_element_type=jnp.float32).astype(jnp.bfloat16)
        expert_in = expert_in.reshape(n_ing, local_e, n_grp, cap_expert, hidden)
        in_gate = jnp.transpose(slot_gate, (1, 0, 2)).reshape(n_ing, local_e, n_grp, cap_expert)
        exp_x = lax.all_to_all(expert_in, 'ing', 0, 0, tiled=True)
        exp_gate = lax.all_to_all(in_gate, 'ing', 0, 0, tiled=True)

        act_a = jnp.einsum('ilscd,ldf->ilscf', exp_x, w_one, preferred_element_type=jnp.float32)
        act_b = jnp.einsum('ilscd,ldf->ilscf', exp_x, w_three, preferred_element_type=jnp.float32)
        hidden_act = (jax.nn.silu(act_a) * act_b).astype(jnp.bfloat16)
        expert_out = jnp.einsum('ilscf,lfd->ilscd', hidden_act, w_two, preferred_element_type=jnp.float32)
        scaled = (expert_out * exp_gate[..., None]).astype(jnp.bfloat16)

        returned = lax.all_to_all(scaled, 'ing', 0, 0, tiled=True).reshape(per_group, n_grp, cap_expert, hidden)
        group_sum = jnp.einsum('secr,escd->srd', disp_bf, returned, preferred_element_type=jnp.float32).astype(jnp.bfloat16)
        group_back = lax.all_to_all(group_sum, 'grp', 0, 0, tiled=True)
        return jnp.einsum('hsu,hse->ue', send_bf, group_back, preferred_element_type=jnp.float32).astype(jnp.bfloat16)

    def body(x_first, ids_first, gates_first, x_second, ids_second, gates_second, w_one, w_three, w_two):
        y_first = moe_local(x_first, ids_first, gates_first, w_one, w_three, w_two)
        y_second = moe_local(x_second, ids_second, gates_second, w_one, w_three, w_two)
        return y_first, y_second

    return jax.shard_map(body, mesh=mesh, in_specs=(tok_spec,) * 6 + (w_spec,) * 3, out_specs=(tok_spec, tok_spec), check_vma=False)
```

profile of v0, /device:TPU:97, one launch (start us, length us, event | category | flops | bytes accessed | tf_op | source)
XLA Modules:
  0.0 1855.1 jit_solution(6643174712972663760)
XLA Ops:
  6.8 14.0 fusion.19
  31.4 14.0 fusion.7
  99.3 24.7 %fusion.78 = bf16[8,768,1024]{2,1,0:T(8,128)(2,1)} fusion(s32[8,1536]{1,0:T(8,128)} %bitcast.266, pred[8,1536]{1,0:T(8,128)(4,1)} %bitcast.277, bf16[1536,1024]{1,0:T(8,128)(2,1)S(1)} %copy-done), kind=kOutput, calls=%fused_computation.80 | convolution fusion | flops 19352518656 | bytes 15790080 | tf_op jit(solution)/shard_map/hsu,ue->hse/dot_general | solution.py:29
  131.0 23.8 %fusion.81 = bf16[8,768,1024]{2,1,0:T(8,128)(2,1)} fusion(s32[8,1536]{1,0:T(8,128)S(1)} %bitcast.269, pred[8,1536]{1,0:T(8,128)(4,1)S(1)} %bitcast.274, bf16[1536,1024]{1,0:T(8,128)(2,1)S(1)} %copy-done.23), kind=kOutput, calls=%fused_computation.81 | convolution fusion | flops 19352518656 | bytes 15790080 | tf_op jit(solution)/shard_map/hsu,ue->hse/dot_general | solution.py:29
  154.8 114.7 %all-to-all-done.7 = bf16[8,768,1024]{2,1,0:T(8,128)(2,1)} async-done(((bf16[8,768,1024]{2,1,0:T(8,128)(2,1)}), bf16[8,768,1024]{2,1,0:T(8,128)(2,1)}, u32[]{:S(2)}, u32[]{:S(2)}) %all-to-all-start.7) | async-done | bytes 12582944 | tf_op jit(solution)/shard_map/all_to_all | solution.py:31
  275.8 36.8 %convert_bitcast_fusion = bf16[4,1,8,384,1024]{3,4,0,2,1:T(8,128)(2,1)} fusion(s32[8,4,768]{2,1,0:T(4,128)S(1)} %copy-done.2, pred[8,4,768]{2,1,0:T(4,128)(4,1)S(1)} %copy.159, bf16[8,768,1024]{2,1,0:T(8,128)(2,1)} %all-to-all-done.7), kind=kOutput, calls=%fused_computation.54 | convolution fusion | flops 19358810112 | bytes 37871616 | tf_op jit(solution)/shard_map/secr,srd->escd/dot_general | solution.py:41
  312.6 20.7 %copy.165 = bf16[4,1,8,384,1024]{3,4,2,1,0:T(8,128)(2,1)} copy(bf16[4,1,8,384,1024]{3,4,0,2,1:T(8,128)(2,1)} %convert_bitcast_fusion) | data formatting | bytes 50331648 | tf_op jit(solution)/shard_map/reshape | solution.py:42
  333.3 81.1 %all-to-all-done.1 = bf16[8,768,1024]{2,1,0:T(8,128)(2,1)} async-done(((bf16[8,768,1024]{2,1,0:T(8,128)(2,1)}), bf16[8,768,1024]{2,1,0:T(8,128)(2,1)}, u32[]{:S(2)}, u32[]{:S(2)}) %all-to-all-start.1) | async-done | bytes 12582944 | tf_op jit(solution)/shard_map/all_to_all | solution.py:31
  423.0 36.8 %convert_bitcast_fusion.1 = bf16[4,1,8,384,1024]{3,4,0,2,1:T(8,128)(2,1)} fusion(s32[8,4,768]{2,1,0:T(4,128)S(1)} %copy-done.5, pred[8,4,768]{2,1,0:T(4,128)(4,1)S(1)} %copy-done.19, bf16[8,768,1024]{2,1,0:T(8,128)(2,1)} %all-to-all-done.1), kind=kOutput, calls=%fused_computation.55 | convolution fusion | flops 19358810112 | bytes 37871616 | tf_op jit(solution)/shard_map/secr,srd->escd/dot_general | solution.py:41
  459.8 20.7 %copy.150 = bf16[4,1,8,384,1024]{3,4,2,1,0:T(8,128)(2,1)} copy(bf16[4,1,8,384,1024]{3,4,0,2,1:T(8,128)(2,1)} %convert_bitcast_fusion.1) | data formatting | bytes 50331648 | tf_op jit(solution)/shard_map/reshape | solution.py:42
  480.4 215.3 %all-to-all-done.8 = bf16[4,1,8,384,1024]{3,4,2,1,0:T(8,128)(2,1)} async-done(((bf16[4,1,8,384,1024]{3,4,2,1,0:T(8,128)(2,1)}), bf16[4,1,8,384,1024]{3,4,2,1,0:T(8,128)(2,1)}, u32[]{:S(2)}, u32[]{:S(2)}) %all-to-all-start.8) | async-done | bytes 25165856 | tf_op jit(solution)/shard_map/all_to_all | solution.py:44
  704.7 22.7 %fusion.28 = f32[4,8,384,512]{3,2,1,0:T(8,128)} fusion(bf16[4,1,8,384,1024]{3,4,2,1,0:T(8,128)(2,1)} %all-to-all-done.8, bf16[1,1024,512]{2,1,0:T(8,128)(2,1)S(1)} %copy-done.24), kind=kOutput, calls=%fused_computation.26 | convolution fusion | flops 12884901888 | bytes 51380224 | tf_op jit(solution)/shard_map/ilscd,ldf->ilscf/dot_general | solution.py:48
  727.4 36.4 %fusion.27 = bf16[4,1,8,384,1024]{4,3,2,1,0:T(8,128)(2,1)} fusion(f32[4,8,384]{2,1,0:T(8,128)} %bitcast.66, f32[4,8,384,512]{3,2,1,0:T(8,128)} %fusion.28, bf16[4,1,8,384,1024]{3,4,2,1,0:T(8,128)(2,1)} %all-to-all-done.8, bf16[1,512,1024]{2,1,0:T(8,128)(2,1)S(1)} %copy-done.25, bf16[1,1024,512]{2,1,0:T(8,128)(2,1)} %param.15), kind=kOutput, calls=%fused_computation.25 | convolution fusion | flops 25832718336 | bytes 77643776 | tf_op jit(solution)/shard_map/ilscf,lfd->ilscd/dot_general | solution.py:50
  763.8 212.4 %all-to-all-done.2 = bf16[4,1,8,384,1024]{3,4,2,1,0:T(8,128)(2,1)} async-done(((bf16[4,1,8,384,1024]{3,4,2,1,0:T(8,128)(2,1)}), bf16[4,1,8,384,1024]{3,4,2,1,0:T(8,128)(2,1)}, u32[]{:S(2)}, u32[]{:S(2)}) %all-to-all-start.2) | async-done | bytes 25165856 | tf_op jit(solution)/shard_map/all_to_all | solution.py:44
  985.0 22.6 %fusion.32 = f32[4,8,384,512]{3,2,1,0:T(8,128)} fusion(bf16[4,1,8,384,1024]{3,4,2,1,0:T(8,128)(2,1)} %all-to-all-done.2, bf16[1,1024,512]{2,1,0:T(8,128)(2,1)S(1)} %copy-done.24), kind=kOutput, calls=%fused_computation.30 | convolution fusion | flops 12884901888 | bytes 51380224 | tf_op jit(solution)/shard_map/ilscd,ldf->ilscf/dot_general | solution.py:48
  1007.6 36.4 %fusion.26 = bf16[4,1,8,384,1024]{4,3,2,1,0:T(8,128)(2,1)} fusion(f32[4,8,384]{2,1,0:T(8,128)S(1)} %bitcast.279, f32[4,8,384,512]{3,2,1,0:T(8,128)} %fusion.32, bf16[4,1,8,384,1024]{3,4,2,1,0:T(8,128)(2,1)} %all-to-all-done.2, bf16[1,512,1024]{2,1,0:T(8,128)(2,1)S(1)} %copy-done.25, bf16[1,1024,512]{2,1,0:T(8,128)(2,1)} %param.15), kind=kOutput, calls=%fused_computation.24 | convolution fusion | flops 25832718336 | bytes 77643776 | tf_op jit(solution)/shard_map/ilscf,lfd->ilscd/dot_general | solution.py:50
  1044.0 211.5 %all-to-all-done.10 = bf16[4,1,8,384,1024]{4,3,2,1,0:T(8,128)(2,1)} async-done(((bf16[4,1,8,384,1024]{4,3,2,1,0:T(8,128)(2,1)}), bf16[4,1,8,384,1024]{4,3,2,1,0:T(8,128)(2,1)}, u32[]{:S(2)}, u32[]{:S(2)}) %all-to-all-start.10) | async-done | bytes 25165856 | tf_op jit(solution)/shard_map/all_to_all | solution.py:53
  1264.3 25.1 %bitcast_convert_fusion = bf16[8,768,1024]{2,1,0:T(8,128)(2,1)} fusion(bf16[4,1,8,384,1024]{4,3,2,1,0:T(8,128)(2,1)} %all-to-all-done.10, s32[8,4,768]{2,1,0:T(4,128)S(1)} %copy-done.3, pred[8,4,768]{2,1,0:T(4,128)(4,1)S(1)} %copy-done.17), kind=kOutput, calls=%fused_computation.38 | convolution fusion | flops 19352518656 | bytes 37871616 | tf_op jit(solution)/shard_map/secr,escd->srd/dot_general | solution.py:54
  1289.4 244.5 %all-to-all-done.4 = bf16[4,1,8,384,1024]{4,3,2,1,0:T(8,128)(2,1)} async-done(((bf16[4,1,8,384,1024]{4,3,2,1,0:T(8,128)(2,1)}), bf16[4,1,8,384,1024]{4,3,2,1,0:T(8,128)(2,1)}, u32[]{:S(2)}, u32[]{:S(2)}) %all-to-all-start.4) | async-done | bytes 25165856 | tf_op jit(solution)/shard_map/all_to_all | solution.py:53
  1544.0 25.1 %bitcast_convert_fusion.1 = bf16[8,768,1024]{2,1,0:T(8,128)(2,1)} fusion(bf16[4,1,8,384,1024]{4,3,2,1,0:T(8,128)(2,1)} %all-to-all-done.4, s32[8,4,768]{2,1,0:T(4,128)S(1)} %copy-done.6, pred[8,4,768]{2,1,0:T(4,128)(4,1)S(1)} %copy-done.20), kind=kOutput, calls=%fused_computation.45 | convolution fusion | flops 19352518656 | bytes 37871616 | tf_op jit(solution)/shard_map/secr,escd->srd/dot_general | solution.py:54
  1569.1 113.4 %all-to-all-done.11 = bf16[8,768,1024]{2,1,0:T(8,128)(2,1)} async-done(((bf16[8,768,1024]{2,1,0:T(8,128)(2,1)}), bf16[8,768,1024]{2,1,0:T(8,128)(2,1)}, u32[]{:S(2)}, u32[]{:S(2)}) %all-to-all-start.11) | async-done | bytes 12582944 | tf_op jit(solution)/shard_map/all_to_all | solution.py:55
  1705.8 24.2 %bitcast_convert_fusion.2 = bf16[1536,1024]{1,0:T(8,128)(2,1)} fusion(bf16[8,768,1024]{2,1,0:T(8,128)(2,1)} %all-to-all-done.11, pred[8,768,1536]{1,2,0:T(32,128)(4,1)S(1)} %fusion.141), kind=kOutput, calls=%fused_computation.82 | convolution fusion | flops 19328925696 | bytes 25165824 | tf_op jit(solution)/shard_map/hsu,hse->ue/dot_general | solution.py:56
  1730.0 97.7 %all-to-all-done.5 = bf16[8,768,1024]{2,1,0:T(8,128)(2,1)} async-done(((bf16[8,768,1024]{2,1,0:T(8,128)(2,1)}), bf16[8,768,1024]{2,1,0:T(8,128)(2,1)}, u32[]{:S(2)}, u32[]{:S(2)}) %all-to-all-start.5) | async-done | bytes 12582944 | tf_op jit(solution)/shard_map/all_to_all | solution.py:55
  1827.7 26.9 %bitcast_convert_fusion.3 = bf16[1536,1024]{1,0:T(8,128)(2,1)} fusion(bf16[8,768,1024]{2,1,0:T(8,128)(2,1)} %all-to-all-done.5, pred[8,768,1536]{1,2,0:T(32,128)(4,1)} %fusion.143), kind=kOutput, calls=%fused_computation.83 | convolution fusion | flops 19328925696 | bytes 25165824 | tf_op jit(solution)/shard_map/hsu,hse->ue/dot_general | solution.py:56
  (114 shorter events, 152.0 us)
Async XLA Ops:
  2.1 128.8 %copy-start.12 = (pred[1536,8]{0,1:T(8,128)(4,1)}, pred[1536,8]{0,1:T(8,128)(4,1)S(1)}, u32[]{:S(2)}) copy-start(pred[1536,8]{0,1:T(8,128)(4,1)S(1)} %get-tuple-element.3) | copy-start | bytes 36868
  20.7 24.6 %all-to-all-start.6 = ((f32[8,768,4]{1,2,0:T(4,128)}), f32[8,768,4]{1,2,0:T(4,128)S(1)}, u32[]{:S(2)}, u32[]{:S(2)}) async-start(f32[8,768,4]{1,2,0:T(4,128)} %fusion.19), calls=%async_computation.6 | async-start | bytes 196608 | tf_op jit(solution)/shard_map/all_to_all | solution.py:32
  45.4 24.9 %all-to-all-start = ((f32[8,768,4]{1,2,0:T(4,128)}), f32[8,768,4]{1,2,0:T(4,128)S(1)}, u32[]{:S(2)}, u32[]{:S(2)}) async-start(f32[8,768,4]{1,2,0:T(4,128)} %fusion.7), calls=%async_computation | async-start | bytes 196608 | tf_op jit(solution)/shard_map/all_to_all | solution.py:32
  60.2 215.7 %copy-start.16 = (pred[8,4,768]{2,1,0:T(4,128)(4,1)}, pred[8,4,768]{2,1,0:T(4,128)(4,1)S(1)}, u32[]{:S(2)}) copy-start(pred[8,4,768]{2,1,0:T(4,128)(4,1)S(1)} %copy.159) | copy-start | bytes 73732
  70.3 24.5 %all-to-all-start.9 = ((f32[4,1,8,384]{3,2,1,0:T(8,128)}), f32[4,1,8,384]{3,2,1,0:T(8,128)}, u32[]{:S(2)}, u32[]{:S(2)}) async-start(f32[4,1,8,384]{3,2,1,0:T(8,128)} %copy.167), calls=%async_computation.9 | async-start | bytes 98304 | tf_op jit(solution)/shard_map/all_to_all | solution.py:45
  94.8 29.3 %all-to-all-start.3 = ((f32[4,1,8,384]{3,2,1,0:T(8,128)}), f32[4,1,8,384]{3,2,1,0:T(8,128)S(1)}, u32[]{:S(2)}, u32[]{:S(2)}) async-start(f32[4,1,8,384]{3,2,1,0:T(8,128)} %copy.152), calls=%async_computation.3 | async-start | bytes 98304 | tf_op jit(solution)/shard_map/all_to_all | solution.py:45
  124.7 144.8 %all-to-all-start.7 = ((bf16[8,768,1024]{2,1,0:T(8,128)(2,1)}), bf16[8,768,1024]{2,1,0:T(8,128)(2,1)}, u32[]{:S(2)}, u32[]{:S(2)}) async-start(bf16[8,768,1024]{2,1,0:T(8,128)(2,1)} %fusion.78), calls=%async_computation.7 | async-start | bytes 25165824 | tf_op jit(solution)/shard_map/all_to_all | solution.py:31
  154.8 121.1 %copy-start.2 = (s32[8,4,768]{2,1,0:T(4,128)S(1)}, s32[8,4,768]{2,1,0:T(4,128)}, u32[]{:S(2)}) copy-start(s32[8,4,768]{2,1,0:T(4,128)} %reshape.175) | copy-start | bytes 294916
  269.5 144.9 %all-to-all-start.1 = ((bf16[8,768,1024]{2,1,0:T(8,128)(2,1)}), bf16[8,768,1024]{2,1,0:T(8,128)(2,1)}, u32[]{:S(2)}, u32[]{:S(2)}) async-start(bf16[8,768,1024]{2,1,0:T(8,128)(2,1)} %fusion.81), calls=%async_computation.1 | async-start | bytes 25165824 | tf_op jit(solution)/shard_map/all_to_all | solution.py:31
  414.4 281.3 %all-to-all-start.8 = ((bf16[4,1,8,384,1024]{3,4,2,1,0:T(8,128)(2,1)}), bf16[4,1,8,384,1024]{3,4,2,1,0:T(8,128)(2,1)}, u32[]{:S(2)}, u32[]{:S(2)}) async-start(bf16[4,1,8,384,1024]{3,4,2,1,0:T(8,128)(2,1)} %copy.165), calls=%async_computation.8 | async-start | bytes 50331648 | tf_op jit(solution)/shard_map/all_to_all | solution.py:44
  480.4 224.2 %copy-start.24 = (bf16[1,1024,512]{2,1,0:T(8,128)(2,1)S(1)}, bf16[1,1024,512]{2,1,0:T(8,128)(2,1)}, u32[]{:S(2)}) copy-start(bf16[1,1024,512]{2,1,0:T(8,128)(2,1)} %param.16) | copy-start | bytes 3145732
  695.7 280.5 %all-to-all-start.2 = ((bf16[4,1,8,384,1024]{3,4,2,1,0:T(8,128)(2,1)}), bf16[4,1,8,384,1024]{3,4,2,1,0:T(8,128)(2,1)}, u32[]{:S(2)}, u32[]{:S(2)}) async-start(bf16[4,1,8,384,1024]{3,4,2,1,0:T(8,128)(2,1)} %copy.150), calls=%async_computation.2 | async-start | bytes 50331648 | tf_op jit(solution)/shard_map/all_to_all | solution.py:44
  976.2 279.3 %all-to-all-start.10 = ((bf16[4,1,8,384,1024]{4,3,2,1,0:T(8,128)(2,1)}), bf16[4,1,8,384,1024]{4,3,2,1,0:T(8,128)(2,1)}, u32[]{:S(2)}, u32[]{:S(2)}) async-start(bf16[4,1,8,384,1024]{4,3,2,1,0:T(8,128)(2,1)} %fusion.27), calls=%async_computation.10 | async-start | bytes 50331648 | tf_op jit(solution)/shard_map/all_to_all | solution.py:53
  1044.0 220.3 %copy-start.3 = (s32[8,4,768]{2,1,0:T(4,128)S(1)}, s32[8,4,768]{2,1,0:T(4,128)}, u32[]{:S(2)}) copy-start(s32[8,4,768]{2,1,0:T(4,128)} %reshape.175) | copy-start | bytes 294916
  1044.0 220.3 %copy-start.17 = (pred[8,4,768]{2,1,0:T(4,128)(4,1)S(1)}, pred[8,4,768]{2,1,0:T(4,128)(4,1)}, u32[]{:S(2)}) copy-start(pred[8,4,768]{2,1,0:T(4,128)(4,1)} %copy-done.16) | copy-start | bytes 73732
  1255.6 278.4 %all-to-all-start.4 = ((bf16[4,1,8,384,1024]{4,3,2,1,0:T(8,128)(2,1)}), bf16[4,1,8,384,1024]{4,3,2,1,0:T(8,128)(2,1)}, u32[]{:S(2)}, u32[]{:S(2)}) async-start(bf16[4,1,8,384,1024]{4,3,2,1,0:T(8,128)(2,1)} %fusion.26), calls=%async_computation.4 | async-start | bytes 50331648 | tf_op jit(solution)/shard_map/all_to_all | solution.py:53
  1289.4 254.5 %copy-start.6 = (s32[8,4,768]{2,1,0:T(4,128)S(1)}, s32[8,4,768]{2,1,0:T(4,128)}, u32[]{:S(2)}) copy-start(s32[8,4,768]{2,1,0:T(4,128)} %copy-done.4) | copy-start | bytes 294916
  1289.4 254.5 %copy-start.20 = (pred[8,4,768]{2,1,0:T(4,128)(4,1)S(1)}, pred[8,4,768]{2,1,0:T(4,128)(4,1)}, u32[]{:S(2)}) copy-start(pred[8,4,768]{2,1,0:T(4,128)(4,1)} %copy-done.18) | copy-start | bytes 73732
  1533.9 148.6 %all-to-all-start.11 = ((bf16[8,768,1024]{2,1,0:T(8,128)(2,1)}), bf16[8,768,1024]{2,1,0:T(8,128)(2,1)}, u32[]{:S(2)}, u32[]{:S(2)}) async-start(bf16[8,768,1024]{2,1,0:T(8,128)(2,1)} %bitcast_convert_fusion), calls=%async_computation.11 | async-start | bytes 25165824 | tf_op jit(solution)/shard_map/all_to_all | solution.py:55
  1569.1 120.1 %copy-start.8 = (s32[1,8,12,128]{3,1,2,0:T(8,128)S(1)}, s32[1,8,12,128]{3,1,2,0:T(8,128)}, u32[]{:S(2)}) copy-start(s32[1,8,12,128]{3,1,2,0:T(8,128)} %copy-done.7) | copy-start | bytes 147460
  1569.1 120.1 %copy-start.15 = (pred[1536,8]{0,1:T(8,128)(4,1)S(1)}, pred[1536,8]{0,1:T(8,128)(4,1)}, u32[]{:S(2)}) copy-start(pred[1536,8]{0,1:T(8,128)(4,1)} %copy-done.14) | copy-start | bytes 36868
  1569.1 127.9 %copy-start.11 = (s32[1,8,12,128]{3,1,2,0:T(8,128)S(1)}, s32[1,8,12,128]{3,1,2,0:T(8,128)}, u32[]{:S(2)}) copy-start(s32[1,8,12,128]{3,1,2,0:T(8,128)} %copy-done.9) | copy-start | bytes 147460
  1569.1 127.9 %copy-start.13 = (pred[1536,8]{0,1:T(8,128)(4,1)S(1)}, pred[1536,8]{0,1:T(8,128)(4,1)}, u32[]{:S(2)}) copy-start(pred[1536,8]{0,1:T(8,128)(4,1)} %copy-done.12) | copy-start | bytes 36868
  1682.5 145.1 %all-to-all-start.5 = ((bf16[8,768,1024]{2,1,0:T(8,128)(2,1)}), bf16[8,768,1024]{2,1,0:T(8,128)(2,1)}, u32[]{:S(2)}, u32[]{:S(2)}) async-start(bf16[8,768,1024]{2,1,0:T(8,128)(2,1)} %bitcast_convert_fusion.1), calls=%async_computation.5 | async-start | bytes 25165824 | tf_op jit(solution)/shard_map/all_to_all | solution.py:55
  (14 other events, 492.6 us)
where the time goes:
time: 1860 us
  waiting for transfers between devices  1290 us (69%)
  matrix products  370 us (20%)
  starting transfers between devices  86.1 us (5%)
  other arithmetic  58.2 us (3%)
  local copies, waits for them, and re-layouts  49 us (3%)
    all_to_all x2, waiting for transfers between devices, moe_local(): lax.all_to_all(scaled, 'ing', 0, 0, tiled=True)  456 us
    all_to_all x2, waiting for transfers between devices, moe_local(): exp_x = lax.all_to_all(expert_in, 'ing', 0, 0, tiled=True)  428 us
    all_to_all x2, waiting for transfers between devices, moe_local(): group_back = lax.all_to_all(group_sum, 'grp', 0, 0, tiled=True)  211 us
    all_to_all x2, waiting for transfers between devices, moe_local(): recv_x = lax.all_to_all(send_x, 'grp', 0, 0, tiled=True)  196 us
    dot_general x2, matrix products, moe_local(): jnp.einsum('secr,srd->escd', disp_bf, recv_x, preferred_element_type=jnp....  73.6 us
    dot_general x2, matrix products, moe_local(): jnp.einsum('ilscf,lfd->ilscd', hidden_act, w_two, preferred_element_type=...  72.8 us
    dot_general x2, matrix products, moe_local(): jnp.einsum('hsu,hse->ue', send_bf, group_back, preferred_element_type=jnp...  51.1 us
    dot_general x2, matrix products, moe_local(): jnp.einsum('secr,escd->srd', disp_bf, returned, preferred_element_type=jn...  50.3 us
  transfers between devices with their start and end apart: 12, of which 8 were waited for; matrix products, arithmetic and copies ran while one was open for 23% of the time, Pallas kernels for 0%

commit v1 on v0

v1 whole, which is shorter than its diff:
```python
import functools

import jax
import jax.numpy as jnp
from jax import lax
from jax.experimental import pallas as pl
from jax.experimental.pallas import tpu as pltpu
from jax.sharding import PartitionSpec as P

MESH = pl.DeviceIdType.MESH
AHEAD = 8
RING = 4
ORDER = [(0, 0), (0, 1), (0, 3), (0, 2), (1, 0), (3, 0), (1, 1), (1, 3), (3, 1), (3, 3), (1, 2), (3, 2), (2, 0), (2, 1), (2, 3), (2, 2)]
GROUP_DX = [0, 0, 1, 1, 3, 3, 2, 2]
UNIT_STEP = {1: 3, 2: 6, 3: 8, 4: 9, 5: 11, 6: 13, 7: 15, 8: 15, 9: 17, 10: 18, 11: 20, 12: 22, 13: 25, 14: 27, 15: 31}


def link_sends():
    lists = []
    for d in (1, -1):
        kf, kg = (0, 2) if d > 0 else (1, 3)
        sends = [(0, 0, k) for k in (0, 1, 2, 3)] + [(-d, 0, kf), (-d, 0, kg)]
        sends += [(0, b, k) for b in (1, -1, 2) for k in (2, 3)] + [(-d, b, kg) for b in (1, -1, 2)]
        lists.append([(a % RING, b % RING, k) for a, b, k in sends])
    for d in (1, -1):
        kf, kg = (0, 2) if d > 0 else (1, 3)
        sends = [(0, 0, k) for k in (2, 3, 0, 1)] + [(0, -d, kg), (0, -d, kf)]
        sends += [(a, 0, k) for a in (1, -1) for k in (0, 1)] + [(a, -d, kf) for a in (1, -1)]
        sends += [(2, 0, 0), (2, 0, 1), (2, -d, kf)]
        lists.append([(a % RING, b % RING, k) for a, b, k in sends])
    return lists


STEP_OF_LINK = [(1, 0), (-1, 0), (0, 1), (0, -1)]


def make_plan():
    sends = link_sends()
    units = len(sends[0])
    shifted = lambda link, item: ((item[0] - STEP_OF_LINK[link][0]) % RING, (item[1] - STEP_OF_LINK[link][1]) % RING, item[2])
    have = {(0, 0, k) for k in range(4)}
    nxt = [0] * 4
    plan = {}
    done = set()
    for unit in range(units + 1):
        arrivals = [] if unit == 0 else [shifted(link, sends[link][unit - 1]) for link in range(4)]
        assert not have & set(arrivals)
        have |= set(arrivals)
        issued = []
        moved = True
        while moved:
            moved = False
            for link in range(4):
                if nxt[link] < units and sends[link][nxt[link]] in have:
                    issued.append((link, nxt[link], sends[link][nxt[link]], shifted(link, sends[link][nxt[link]])))
                    nxt[link] += 1
                    moved = True
        complete = [p for p in ORDER if p not in done and all((*p, k) in have for k in range(4))]
        done |= set(complete)
        plan[unit] = (arrivals, issued, complete)
    assert len(have) == 4 * RING * RING and nxt == [units] * 4
    return plan, units


def pick(index, values):
    out = jnp.int32(values[0])
    for i, v in enumerate(values[1:], 1):
        out = jnp.where(index == i, jnp.int32(v), out)
    return out


def kernel(cap, x_first, x_second, ids_ref, gates_ref, wown, y_first, y_second, wall, zh,
           xv, yacc, wv, xg, gb, zst, zc, slotrow, gaterow, slotcol,
           recv_sem, send_sem, d2d_recv, d2d_send, w_sem, x_sem, z_sem, zl_sem, y_sem):
    grp, y = lax.axis_index('grp'), lax.axis_index('ing')
    x, c = grp // 2, grp % 2
    tokens = xv.shape[1]
    experts = slotrow.shape[1]
    per_group = RING
    plan, units = make_plan()
    npos = RING * RING

    def expert(dx, dy, core):
        return (((x + dx) % RING) * 2 + core) * per_group + (y + dy) % RING

    def neighbour(link):
        sx, sy = STEP_OF_LINK[link]
        return {'grp': ((x + sx) % RING) * 2 + c, 'ing': (y + sy) % RING}

    partner = {'grp': x * 2 + (1 - c), 'ing': y}

    barrier = pltpu.get_barrier_semaphore()
    for dev in [neighbour(link) for link in range(4)] + [partner]:
        pl.semaphore_signal(barrier, inc=1, device_id=dev, device_id_type=MESH)
    pl.semaphore_wait(barrier, 5)

    def quarter_copy(link, slot, item, target):
        dx, dy, k = item
        e = expert(dx, dy, c)
        src = wown.at[:, k] if (dx, dy) == (0, 0) else wall.at[e, :, k]
        return pltpu.make_async_remote_copy(
            src_ref=src, dst_ref=wall.at[e, :, k], send_sem=send_sem.at[link * units + slot],
            recv_sem=recv_sem.at[(target[0] * RING + target[1]) * 4 + k], device_id=neighbour(link), device_id_type=MESH)

    def d2d_copy(pos):
        j = ORDER.index(pos)
        e = expert(*pos, c)
        src = wown if j == 0 else wall.at[e]
        return pltpu.make_async_remote_copy(
            src_ref=src, dst_ref=wall.at[e], send_sem=d2d_send.at[j], recv_sem=d2d_recv.at[j],
            device_id=partner, device_id_type=MESH)

    def act(unit):
        arrivals, issued, complete = plan[unit]
        for dx, dy, k in arrivals:
            ref = wall.at[expert(dx, dy, c), :, k]
            pltpu.make_async_remote_copy(
                src_ref=ref, dst_ref=ref, send_sem=send_sem.at[0], recv_sem=recv_sem.at[(dx * RING + dy) * 4 + k],
                device_id=partner, device_id_type=MESH).wait_recv()
        for link, slot, item, target in issued:
            quarter_copy(link, slot, item, target).start()
        for pos in complete:
            d2d_copy(pos).start()

    act(0)
    x_copies = [pltpu.make_async_copy(src, xv.at[m], x_sem.at[m]) for m, src in enumerate((x_first, x_second))]
    for copy in x_copies:
        copy.start()
    pltpu.make_async_copy(wown, wv.at[0], w_sem.at[0]).start()

    lane_block = 128
    upper = (lax.broadcasted_iota(jnp.int32, (lane_block, lane_block), 0)
             <= lax.broadcasted_iota(jnp.int32, (lane_block, lane_block), 1)).astype(jnp.bfloat16)
    for m in range(2):
        e_iota = lax.broadcasted_iota(jnp.int32, (experts, lane_block), 0)
        carry = jnp.zeros((experts, 1), jnp.float32)
        for b in range(tokens // lane_block):
            cols = pl.ds(b * lane_block, lane_block)
            mem = jnp.zeros((experts, lane_block), jnp.float32)
            gat = jnp.zeros((experts, lane_block), jnp.float32)
            for k in range(ids_ref.shape[1]):
                hit = ids_ref[m, k:k + 1, cols] == e_iota
                mem = jnp.where(hit, 1.0, mem)
                gat = jnp.where(hit, gates_ref[m, k:k + 1, cols], gat)
            total = jnp.dot(mem.astype(jnp.bfloat16), upper, preferred_element_type=jnp.float32) + carry
            carry = total[:, lane_block - 1:]
            slot = jnp.where(mem > 0.0, total - 1.0, -1.0)
            slotrow[m, :, cols] = slot.astype(jnp.int32)
            gaterow[m, :, cols] = gat
            full = jnp.concatenate([slot, jnp.full((lane_block - experts, lane_block), -1.0, jnp.float32)], axis=0)
            slotcol[m, cols, :] = full.T.astype(jnp.int32)

    for m in range(2):
        @pl.loop(0, tokens // 128)
        def _(i):
            yacc[m, pl.ds(i * 128, 128), :] = jnp.zeros((128, yacc.shape[2]), jnp.float32)

    for copy in x_copies:
        copy.wait()

    def step_expert(s):
        j = s // 2
        core = (c + s) % 2
        return expert(pick(j, [p[0] for p in ORDER]), pick(j, [p[1] for p in ORDER]), core)

    def gather(s):
        e = step_expert(s)
        ring = s % AHEAD

        @pl.loop(0, 2)
        def _(m):
            mask = slotrow[m, pl.ds(e, 1), :] == lax.broadcasted_iota(jnp.int32, (cap, tokens), 0)
            gb[ring, m] = jnp.sum(jnp.where(mask, gaterow[m, pl.ds(e, 1), :], 0.0), axis=1, keepdims=True)
            xg[ring, m] = jnp.dot(mask.astype(jnp.bfloat16), xv[m], preferred_element_type=jnp.float32).astype(jnp.bfloat16)

    def z_copy(s):
        e = step_expert(s)
        return pltpu.make_async_copy(zst, zh.at[e // per_group, :, pl.ds((e % per_group) * cap, cap), :], z_sem)

    def ffn(s):
        ring = s % AHEAD
        par = s % 2
        width = wv.shape[4]
        depth = 4 * wv.shape[3]
        pltpu.make_async_copy(wall.at[0], wv.at[par], w_sem.at[par]).wait()

        @pl.loop(0, 2)
        def _(m):
            rows = xg[ring, m]
            act_a = jnp.dot(rows, wv[par, 0].reshape(depth, width), preferred_element_type=jnp.float32)
            act_b = jnp.dot(rows, wv[par, 1].reshape(depth, width), preferred_element_type=jnp.float32)
            hid = (jax.nn.silu(act_a) * act_b).astype(jnp.bfloat16)
            gate = gb[ring, m]
            for half in range(2):
                w2 = wv[par, 2, 2 * half:2 * half + 2].reshape(depth // 2, width)
                out = jnp.dot(hid, w2, preferred_element_type=jnp.float32)
                zst[m, :, half * width:(half + 1) * width] = (out * gate).astype(jnp.bfloat16)
        z_copy(s).start()

    def fetch(s):
        par = s % 2
        for j in range(npos):
            @pl.when(s == 2 * j + 1)
            def _():
                ref = wall.at[expert(*ORDER[j], 1 - c)]
                pltpu.make_async_remote_copy(
                    src_ref=ref, dst_ref=ref, send_sem=d2d_send.at[0], recv_sem=d2d_recv.at[j],
                    device_id=partner, device_id_type=MESH).wait_recv()
        pltpu.make_async_copy(wall.at[step_expert(s)], wv.at[par], w_sem.at[par]).start()

    def combine(base, items):
        def load(i):
            t = base + i // 2
            g = ((x + pick(t, GROUP_DX)) % RING) * 2 + (c + t) % 2
            return g, pltpu.make_async_copy(zh.at[g, i % 2], zc.at[i % 2], zl_sem.at[i % 2])

        load(0)[1].start()
        tile = cap

        @pl.loop(0, items)
        def _(i):
            g, copy = load(i)
            copy.wait()

            @pl.when(i + 1 < items)
            def _():
                load(i + 1)[1].start()

            m = i % 2

            @pl.loop(0, tokens // tile)
            def _(r):
                rows = pl.ds(pl.multiple_of(r * tile, tile), tile)
                table = slotcol[m, rows, :]
                lane = lax.broadcasted_iota(jnp.int32, table.shape, 1)
                lane_cap = lax.broadcasted_iota(jnp.int32, (tile, cap), 1)
                parts = []
                for q in range(per_group):
                    col = jnp.sum(jnp.where(lane == g * per_group + q, table, 0), axis=1, keepdims=True)
                    parts.append((col == lane_cap).astype(jnp.bfloat16))
                sel = jnp.concatenate(parts, axis=1)
                part = jnp.dot(sel, zc[m], preferred_element_type=jnp.float32)
                yacc[m, rows, :] += part.astype(jnp.bfloat16).astype(jnp.float32)

    steps = 2 * npos

    @pl.loop(0, steps + AHEAD)
    def _(v):
        s = v - AHEAD

        @pl.when(s >= 0)
        def _():
            ffn(s)

        for unit in range(1, units + 1):
            @pl.when(v == UNIT_STEP[unit])
            def _():
                act(unit)

        @pl.when((s >= 0) & (s + 1 < steps))
        def _():
            fetch(s + 1)

        @pl.when(v < steps)
        def _():
            gather(v)

        @pl.when(s >= 0)
        def _():
            z_copy(s).wait()

        due = (s == 7) | (s == 23) | (s == 31)

        @pl.when(due)
        def _():
            combine(jnp.where(s == 7, 0, jnp.where(s == 23, 2, 6)), jnp.where(s == 23, 8, 4))

    for m, dst in enumerate((y_first, y_second)):
        @pl.loop(0, tokens // 128)
        def _(i):
            rows = pl.ds(pl.multiple_of(i * 128, 128), 128)
            xv[m, rows, :] = yacc[m, rows, :].astype(jnp.bfloat16)
        pltpu.make_async_copy(xv.at[m], dst, y_sem.at[m]).start()
    for m, dst in enumerate((y_first, y_second)):
        pltpu.make_async_copy(xv.at[m], dst, y_sem.at[m]).wait()

    for unit in range(units + 1):
        _, issued, complete = plan[unit]
        for link, slot, item, target in issued:
            quarter_copy(link, slot, item, target).wait_send()
        for pos in complete:
            d2d_copy(pos).wait_send()


def solution(mesh):
    n_grp = mesh.shape['grp']
    n_ing = mesh.shape['ing']
    assert n_grp == 2 * RING and n_ing == RING
    tok_spec = P(('dp', 'grp', 'ing'), None)
    w_spec = P(('grp', 'ing'), None, None)

    def body(x_first, ids_first, gates_first, x_second, ids_second, gates_second, w_one, w_three, w_two):
        tokens, hidden = x_first.shape
        top_k = ids_first.shape[1]
        experts = n_grp * n_ing
        limit_m = min(top_k, n_grp // 2)
        cap = limit_m * (-(-(tokens * (top_k // limit_m)) // experts))
        inner = w_one.shape[2]
        ids = jnp.stack([ids_first.T, ids_second.T])
        gates = jnp.stack([gates_first.T, gates_second.T])
        quarter = hidden // 4
        w2 = w_two[0].reshape(2, inner // 2, 2, hidden // 2).transpose(2, 0, 1, 3).reshape(4, inner // 2, hidden // 2)
        wown = jnp.stack([w_one[0].reshape(4, quarter, inner), w_three[0].reshape(4, quarter, inner), w2])
        bf, f32, i32 = jnp.bfloat16, jnp.float32, jnp.int32
        hbm = pl.BlockSpec(memory_space=pl.ANY)
        vmem = pl.BlockSpec(memory_space=pltpu.VMEM)
        dma = pltpu.SemaphoreType.DMA
        y_shape = jax.ShapeDtypeStruct((tokens, hidden), bf)
        outs = pl.pallas_call(
            functools.partial(kernel, cap),
            out_shape=(y_shape, y_shape,
                       jax.ShapeDtypeStruct((experts,) + wown.shape, bf),
                       jax.ShapeDtypeStruct((n_grp, 2, n_ing * cap, hidden), bf)),
            in_specs=[hbm, hbm, vmem, vmem, hbm],
            out_specs=(hbm,) * 4,
            scratch_shapes=[
                pltpu.VMEM((2, tokens, hidden), bf),
                pltpu.VMEM((2, tokens, hidden), f32),
                pltpu.VMEM((2,) + wown.shape, bf),
                pltpu.VMEM((AHEAD, 2, cap, hidden), bf),
                pltpu.VMEM((AHEAD, 2, cap, 1), f32),
                pltpu.VMEM((2, cap, hidden), bf),
                pltpu.VMEM((2, n_ing * cap, hidden), bf),
                pltpu.VMEM((2, experts, tokens), i32),
                pltpu.VMEM((2, experts, tokens), f32),
                pltpu.VMEM((2, tokens, 128), i32),
                dma((64,)), dma((60,)), dma((16,)), dma((16,)), dma((2,)), dma((2,)), dma(()), dma((2,)), dma((2,)),
            ],
            compiler_params=pltpu.CompilerParams(collective_id=0, has_side_effects=True, vmem_limit_bytes=67043328),
        )(x_first, x_second, ids, gates, wown)
        return outs[0], outs[1]

    return jax.shard_map(body, mesh=mesh, in_specs=(tok_spec,) * 6 + (w_spec,) * 3, out_specs=(tok_spec, tok_spec), check_vma=False)
```

time: 1860 us -> 409 us (0.22)
  waiting for transfers between devices: 1290 us -> 0 us
  Pallas kernels: 0 us -> 395 us
  matrix products: 370 us -> 0 us
  starting transfers between devices: 86.1 us -> 0 us
  other arithmetic: 58.2 us -> 5.08 us
  local copies, waits for them, and re-layouts: 49 us -> 7.7 us
    all_to_all x12 -> x0, waiting for transfers between devices: 1290 us -> none  [the longest x2 456 us: moe_local(): lax.all_to_all(scaled, 'ing', 0, 0, tiled=True)]
    pallas_call x0 -> x1, Pallas kernels: none -> 395 us  [body(): pl.pallas_call(functools.partial(kernel, cap), out_shape=(y_shape, y_shap...]
    dot_general x14 -> x0, matrix products: 370 us -> none  [the longest x2 73.6 us: moe_local(): jnp.einsum('secr,srd->escd', disp_bf, recv_x, preferred_element_type=jnp....]
    all_to_all x12 -> x0, starting transfers between devices: 86.1 us -> none  [the longest x2 17.5 us: moe_local(): exp_x = lax.all_to_all(expert_in, 'ing', 0, 0, tiled=True)]
    reshape x6 -> x0, local copies, waits for them, and re-layouts: 44.1 us -> none  [the longest x2 41.4 us: moe_local(): expert_in = expert_in.reshape(n_ing, local_e, n_grp, cap_expert, hidden)]
    reduce_sum x4 -> x0, other arithmetic: 20.2 us -> none  [the longest x2 18.2 us: moe_local(): jnp.sum(jnp.where(disp_sel, jnp.swapaxes(recv_gate, 1, 2)[:, :, None, :],...]
  transfers between devices with their start and end apart: 12 -> 0, of which waited for: 8 -> 0; matrix products, arithmetic and copies ran while one was open for 23% -> 0% of each run, Pallas kernels for 0% -> 0%
where the time goes in v1:
time: 409 us; the launch traced here: 408 us
  Pallas kernels  395 us (97%)
  local copies, waits for them, and re-layouts  7.7 us (2%)
  other arithmetic  5.08 us (1%)
    pallas_call x1, Pallas kernels, body(): pl.pallas_call(functools.partial(kernel, cap), out_shape=(y_shape, y_shap...  395 us

profile of v1, /device:TPU:97, one launch (start us, length us, event | category | flops | bytes accessed | tf_op | source)
XLA Modules:
  0.0 408.2 jit_solution(1537190886100513655)
XLA Ops:
  0.6 0.0 copy-start.1
  0.6 0.0 copy-start.2
  0.7 1.6 pad_add_fusion.ids_ref
  2.3 1.5 pad_maximum_fusion.1.gates_ref
  3.7 1.8 reshape_squeeze.3
  5.6 0.2 copy.11
  5.8 0.0 copy-done.1
  5.8 0.0 copy-done.2
  5.8 2.0 pad_maximum_fusion.wown
  7.8 394.7 %shard_map.104 = (bf16[1536,1024]{1,0:T(8,128)(2,1)}, bf16[1536,1024]{1,0:T(8,128)(2,1)}, bf16[32,3,4,256,512]{4,3,2,1,0:T(8,128)(2,1)}, bf16[8,2,1536,1024]{3,2,1,0:T(8,128)(2,1)}) custom-call(bf16[1536,1024]{1,0:T(8,128)(2,1)} %x_first.1, bf16[1536,1024]{1,0:T(8,128)(2,1)} %x_second.1, s32[2,8,1536]{2,1,0:T(8,128)} %pad_add_fusion.ids_ref, ...), custom_call_target="tpu_custom_call" | custom-call | tf_op jit(solution)/shard_map/pallas_call | solution.py:319
  402.5 0.0 copy-start
  402.5 4.0 copy.14
  406.5 0.0 copy-done
  406.5 1.7 copy.15
Async XLA Ops:
  0.6 5.1 %copy-start.1 = (bf16[1,1024,512]{2,1,0:T(8,128)(2,1)S(1)}, bf16[1,1024,512]{2,1,0:T(8,128)(2,1)}, u32[]{:S(2)}) copy-start(bf16[1,1024,512]{2,1,0:T(8,128)(2,1)} %param.16) | copy-start | bytes 3145732
  0.6 5.1 %copy-start.2 = (bf16[1,1024,512]{2,1,0:T(8,128)(2,1)S(1)}, bf16[1,1024,512]{2,1,0:T(8,128)(2,1)}, u32[]{:S(2)}) copy-start(bf16[1,1024,512]{2,1,0:T(8,128)(2,1)} %param.15) | copy-start | bytes 3145732
  402.5 4.0 copy-start

commit v2 on v1

--- a/solution.py
+++ b/solution.py
@@ -8,25 +8,28 @@
 from jax.sharding import PartitionSpec as P
 
 MESH = pl.DeviceIdType.MESH
-AHEAD = 8
+AHEAD = 20
 RING = 4
-ORDER = [(0, 0), (0, 1), (0, 3), (0, 2), (1, 0), (3, 0), (1, 1), (1, 3), (3, 1), (3, 3), (1, 2), (3, 2), (2, 0), (2, 1), (2, 3), (2, 2)]
+ORDER = [(0, 0), (0, 1), (0, 3), (1, 0), (3, 0), (0, 2), (1, 1), (1, 3), (1, 2), (3, 1), (3, 3), (3, 2), (2, 0), (2, 1), (2, 3), (2, 2)]
 GROUP_DX = [0, 0, 1, 1, 3, 3, 2, 2]
-UNIT_STEP = {1: 3, 2: 6, 3: 8, 4: 9, 5: 11, 6: 13, 7: 15, 8: 15, 9: 17, 10: 18, 11: 20, 12: 22, 13: 25, 14: 27, 15: 31}
+UNIT_STEP = {1: (4, 0), 2: (11, 0), 3: (18, 0), 4: (21, 0), 5: (25, 0), 6: (28, 0), 7: (31, 0), 8: (31, 2), 9: (33, 0), 10: (35, 0),
+             11: (37, 2), 12: (39, 0), 13: (43, 1), 14: (43, 2), 15: (47, 0)}
 
 
 def link_sends():
     lists = []
     for d in (1, -1):
         kf, kg = (0, 2) if d > 0 else (1, 3)
-        sends = [(0, 0, k) for k in (0, 1, 2, 3)] + [(-d, 0, kf), (-d, 0, kg)]
-        sends += [(0, b, k) for b in (1, -1, 2) for k in (2, 3)] + [(-d, b, kg) for b in (1, -1, 2)]
+        pair = (2, 3) if d > 0 else (3, 2)
+        sends = [(0, 0, k) for k in (0, 1, 2, 3)] + [(0, b, k) for b in (1, -1, 2) for k in pair]
+        sends += [(-d, 0, kf), (-d, 0, kg)] + [(-d, b, kg) for b in (1, -1, 2)]
         lists.append([(a % RING, b % RING, k) for a, b, k in sends])
     for d in (1, -1):
         kf, kg = (0, 2) if d > 0 else (1, 3)
+        pair = (0, 1) if d > 0 else (1, 0)
         sends = [(0, 0, k) for k in (2, 3, 0, 1)] + [(0, -d, kg), (0, -d, kf)]
-        sends += [(a, 0, k) for a in (1, -1) for k in (0, 1)] + [(a, -d, kf) for a in (1, -1)]
-        sends += [(2, 0, 0), (2, 0, 1), (2, -d, kf)]
+        for a in (1, -1, 2):
+            sends += [(a, 0, k) for k in pair] + [(a, -d, kf)]
         lists.append([(a % RING, b % RING, k) for a, b, k in sends])
     return lists
 
@@ -69,14 +72,15 @@
     return out
 
 
-def kernel(cap, x_first, x_second, ids_ref, gates_ref, wown, y_first, y_second, wall, zh,
-           xv, yacc, wv, xg, gb, zst, zc, slotrow, gaterow, slotcol,
-           recv_sem, send_sem, d2d_recv, d2d_send, w_sem, x_sem, z_sem, zl_sem, y_sem):
+def kernel(cap, x_first, x_second, ids_ref, gates_ref, wown, y_first, y_second, wall, zh, xh,
+           xv, yacc, w13, w2v, xs, xg, gb, zst, zc, slotrow, gaterow, slotcol,
+           recv_sem, send_sem, d2d_recv, d2d_send, w_sem, x_sem, xo_sem, xi_sem, z_sem, zl_sem, y_sem):
     grp, y = lax.axis_index('grp'), lax.axis_index('ing')
     x, c = grp // 2, grp % 2
     tokens = xv.shape[1]
     experts = slotrow.shape[1]
     per_group = RING
+    width = wown.shape[3]
     plan, units = make_plan()
     npos = RING * RING
 
@@ -126,7 +130,15 @@
     x_copies = [pltpu.make_async_copy(src, xv.at[m], x_sem.at[m]) for m, src in enumerate((x_first, x_second))]
     for copy in x_copies:
         copy.start()
-    pltpu.make_async_copy(wown, wv.at[0], w_sem.at[0]).start()
+
+    def weight_copies(src, par):
+        for half in range(2):
+            yield pltpu.make_async_copy(src.at[half], w13.at[par, :, :, pl.ds(half * width, width)], w_sem.at[par * 4 + half])
+        for half in range(2):
+            yield pltpu.make_async_copy(src.at[2, pl.ds(2 * half, 2)], w2v.at[par, :, :, pl.ds(half * width, width)], w_sem.at[par * 4 + 2 + half])
+
+    for copy in weight_copies(wown, 0):
+        copy.start()
 
     lane_block = 128
     upper = (lax.broadcasted_iota(jnp.int32, (lane_block, lane_block), 0)
@@ -150,6 +162,7 @@
             full = jnp.concatenate([slot, jnp.full((lane_block - experts, lane_block), -1.0, jnp.float32)], axis=0)
             slotcol[m, cols, :] = full.T.astype(jnp.int32)
 
+    gb[...] = jnp.zeros_like(gb)
     for m in range(2):
         @pl.loop(0, tokens // 128)
         def _(i):
@@ -165,40 +178,41 @@
 
     def gather(s):
         e = step_expert(s)
-        ring = s % AHEAD
-
-        @pl.loop(0, 2)
-        def _(m):
+        lane = lax.broadcasted_iota(jnp.int32, (cap, gb.shape[2]), 1)
+        for m in range(2):
             mask = slotrow[m, pl.ds(e, 1), :] == lax.broadcasted_iota(jnp.int32, (cap, tokens), 0)
-            gb[ring, m] = jnp.sum(jnp.where(mask, gaterow[m, pl.ds(e, 1), :], 0.0), axis=1, keepdims=True)
-            xg[ring, m] = jnp.dot(mask.astype(jnp.bfloat16), xv[m], preferred_element_type=jnp.float32).astype(jnp.bfloat16)
+            gate = jnp.sum(jnp.where(mask, gaterow[m, pl.ds(e, 1), :], 0.0), axis=1, keepdims=True)
+            gb[m] = jnp.where(lane == s, gate, gb[m])
+            xs[s % 2, m * cap:(m + 1) * cap, :] = jnp.dot(
+                mask.astype(jnp.bfloat16), xv[m], preferred_element_type=jnp.float32).astype(jnp.bfloat16)
+
+    def row_out(s):
+        return pltpu.make_async_copy(xs.at[s % 2], xh.at[s], xo_sem.at[s % 2])
+
+    def row_in(s):
+        return pltpu.make_async_copy(xh.at[s], xg.at[s % 2], xi_sem.at[s % 2])
 
     def z_copy(s):
         e = step_expert(s)
-        return pltpu.make_async_copy(zst, zh.at[e // per_group, :, pl.ds((e % per_group) * cap, cap), :], z_sem)
+        return pltpu.make_async_copy(zst.at[s % 2], zh.at[e // per_group, :, pl.ds((e % per_group) * cap, cap), :], z_sem.at[s % 2])
 
     def ffn(s):
-        ring = s % AHEAD
         par = s % 2
-        width = wv.shape[4]
-        depth = 4 * wv.shape[3]
-        pltpu.make_async_copy(wall.at[0], wv.at[par], w_sem.at[par]).wait()
-
-        @pl.loop(0, 2)
-        def _(m):
-            rows = xg[ring, m]
-            act_a = jnp.dot(rows, wv[par, 0].reshape(depth, width), preferred_element_type=jnp.float32)
-            act_b = jnp.dot(rows, wv[par, 1].reshape(depth, width), preferred_element_type=jnp.float32)
-            hid = (jax.nn.silu(act_a) * act_b).astype(jnp.bfloat16)
-            gate = gb[ring, m]
-            for half in range(2):
-                w2 = wv[par, 2, 2 * half:2 * half + 2].reshape(depth // 2, width)
-                out = jnp.dot(hid, w2, preferred_element_type=jnp.float32)
-                zst[m, :, half * width:(half + 1) * width] = (out * gate).astype(jnp.bfloat16)
-        z_copy(s).start()
+        rows = xg[par]
+        both = jnp.dot(rows, w13[par].reshape(-1, 2 * width), preferred_element_type=jnp.float32)
+        hid = (jax.nn.silu(both[:, :width]) * both[:, width:]).astype(jnp.bfloat16)
+        out = jnp.dot(hid, w2v[par].reshape(width, -1), preferred_element_type=jnp.float32)
+        lane = lax.broadcasted_iota(jnp.int32, (cap, gb.shape[2]), 1)
+        for m in range(2):
+            gate = jnp.sum(jnp.where(lane == s, gb[m], 0.0), axis=1, keepdims=True)
+            zst[par, m] = (out[m * cap:(m + 1) * cap] * gate).astype(jnp.bfloat16)
+
+    def ready(s):
+        for copy in weight_copies(wown, s % 2):
+            copy.wait()
+        row_in(s).wait()
 
     def fetch(s):
-        par = s % 2
         for j in range(npos):
             @pl.when(s == 2 * j + 1)
             def _():
@@ -206,16 +220,22 @@
                 pltpu.make_async_remote_copy(
                     src_ref=ref, dst_ref=ref, send_sem=d2d_send.at[0], recv_sem=d2d_recv.at[j],
                     device_id=partner, device_id_type=MESH).wait_recv()
-        pltpu.make_async_copy(wall.at[step_expert(s)], wv.at[par], w_sem.at[par]).start()
-
-    def combine(base, items):
+
+        @pl.when(s > 0)
+        def _():
+            for copy in weight_copies(wall.at[step_expert(s)], s % 2):
+                copy.start()
+        row_in(s).start()
+
+    def combine(base, groups, finish=None):
+        items = 2 * groups
+
         def load(i):
-            t = base + i // 2
+            t = base + i % groups
             g = ((x + pick(t, GROUP_DX)) % RING) * 2 + (c + t) % 2
-            return g, pltpu.make_async_copy(zh.at[g, i % 2], zc.at[i % 2], zl_sem.at[i % 2])
+            return g, pltpu.make_async_copy(zh.at[g, i // groups], zc.at[i % 2], zl_sem.at[i % 2])
 
         load(0)[1].start()
-        tile = cap
 
         @pl.loop(0, items)
         def _(i):
@@ -226,61 +246,103 @@
             def _():
                 load(i + 1)[1].start()
 
-            m = i % 2
-
-            @pl.loop(0, tokens // tile)
-            def _(r):
-                rows = pl.ds(pl.multiple_of(r * tile, tile), tile)
-                table = slotcol[m, rows, :]
-                lane = lax.broadcasted_iota(jnp.int32, table.shape, 1)
-                lane_cap = lax.broadcasted_iota(jnp.int32, (tile, cap), 1)
-                parts = []
-                for q in range(per_group):
-                    col = jnp.sum(jnp.where(lane == g * per_group + q, table, 0), axis=1, keepdims=True)
-                    parts.append((col == lane_cap).astype(jnp.bfloat16))
-                sel = jnp.concatenate(parts, axis=1)
-                part = jnp.dot(sel, zc[m], preferred_element_type=jnp.float32)
-                yacc[m, rows, :] += part.astype(jnp.bfloat16).astype(jnp.float32)
+            m = i // groups
+            table = slotcol[m]
+            lane = lax.broadcasted_iota(jnp.int32, table.shape, 1)
+            lane_cap = lax.broadcasted_iota(jnp.int32, (tokens, cap), 1)
+            parts = []
+            for q in range(per_group):
+                col = jnp.sum(jnp.where(lane == g * per_group + q, table, 0), axis=1, keepdims=True)
+                parts.append((col == lane_cap).astype(jnp.bfloat16))
+            sel = jnp.concatenate(parts, axis=1)
+            part = jnp.dot(sel, zc[i % 2], preferred_element_type=jnp.float32)
+            yacc[m] += part.astype(jnp.bfloat16).astype(jnp.float32)
+
+            if finish is not None:
+                @pl.when(i % groups == groups - 1)
+                def _():
+                    finish(m)
 
     steps = 2 * npos
+    last = [2 * max(ORDER.index((dx, dy)) for dy in range(RING)) + 1 for dx in (0, 1, 3)]
 
     @pl.loop(0, steps + AHEAD)
     def _(v):
         s = v - AHEAD
 
+        late = (s == last[0]) | (s == last[1]) | (s == last[2])
+
+        @pl.when((v >= 2) & (v < steps + 2))
+        def _():
+            row_out(v - 2).wait()
+
+        drained = (s < 2)
+        for t in last:
+            drained = drained | (s == t + 1) | (s == t + 2)
+
+        @pl.when(jnp.logical_not(drained))
+        def _():
+            z_copy(s - 2).wait()
+
+        def acts(phase):
+            for unit in range(1, units + 1):
+                if UNIT_STEP[unit][1] == phase:
+                    @pl.when(v == UNIT_STEP[unit][0])
+                    def _():
+                        act(unit)
+
+        acts(0)
+
+        @pl.when((s >= -1) & (s + 1 < steps) & jnp.logical_not(late))
+        def _():
+            fetch(s + 1)
+
+        @pl.when(v < AHEAD)
+        def _():
+            gather(v)
+
+        @pl.when((v >= AHEAD) & (v < steps))
+        def _():
+            ready(s)
+            ffn(s)
+            gather(v)
+
+        @pl.when(v >= steps)
+        def _():
+            ready(s)
+            ffn(s)
+
+        @pl.when(v < steps)
+        def _():
+            row_out(v).start()
+
         @pl.when(s >= 0)
         def _():
-            ffn(s)
-
-        for unit in range(1, units + 1):
-            @pl.when(v == UNIT_STEP[unit])
-            def _():
-                act(unit)
-
-        @pl.when((s >= 0) & (s + 1 < steps))
-        def _():
+            z_copy(s).start()
+
+        @pl.when(late)
+        def _():
+            z_copy(s - 1).wait()
+            z_copy(s).wait()
+            acts(1)
+            combine(jnp.where(s == last[0], 0, jnp.where(s == last[1], 2, 4)), 2)
+            acts(2)
             fetch(s + 1)
 
-        @pl.when(v < steps)
-        def _():
-            gather(v)
-
-        @pl.when(s >= 0)
-        def _():
-            z_copy(s).wait()
-
-        due = (s == 7) | (s == 23) | (s == 31)
-
-        @pl.when(due)
-        def _():
-            combine(jnp.where(s == 7, 0, jnp.where(s == 23, 2, 6)), jnp.where(s == 23, 8, 4))
-
-    for m, dst in enumerate((y_first, y_second)):
+    z_copy(steps - 2).wait()
+    z_copy(steps - 1).wait()
+
+    def finish(m):
         @pl.loop(0, tokens // 128)
         def _(i):
             rows = pl.ds(pl.multiple_of(i * 128, 128), 128)
             xv[m, rows, :] = yacc[m, rows, :].astype(jnp.bfloat16)
-        pltpu.make_async_copy(xv.at[m], dst, y_sem.at[m]).start()
+        for n, dst in enumerate((y_first, y_second)):
+            @pl.when(m == n)
+            def _():
+                pltpu.make_async_copy(xv.at[n], dst, y_sem.at[n]).start()
+
+    combine(6, 2, finish)
     for m, dst in enumerate((y_first, y_second)):
         pltpu.make_async_copy(xv.at[m], dst, y_sem.at[m]).wait()
 
@@ -320,21 +382,24 @@
             functools.partial(kernel, cap),
             out_shape=(y_shape, y_shape,
                        jax.ShapeDtypeStruct((experts,) + wown.shape, bf),
-                       jax.ShapeDtypeStruct((n_grp, 2, n_ing * cap, hidden), bf)),
+                       jax.ShapeDtypeStruct((n_grp, 2, n_ing * cap, hidden), bf),
+                       jax.ShapeDtypeStruct((experts, 2 * cap, hidden), bf)),
             in_specs=[hbm, hbm, vmem, vmem, hbm],
-            out_specs=(hbm,) * 4,
+            out_specs=(hbm,) * 5,
             scratch_shapes=[
                 pltpu.VMEM((2, tokens, hidden), bf),
                 pltpu.VMEM((2, tokens, hidden), f32),
-                pltpu.VMEM((2,) + wown.shape, bf),
-                pltpu.VMEM((AHEAD, 2, cap, hidden), bf),
-                pltpu.VMEM((AHEAD, 2, cap, 1), f32),
-                pltpu.VMEM((2, cap, hidden), bf),
+                pltpu.VMEM((2, 4, quarter, 2 * inner), bf),
+                pltpu.VMEM((2, 2, quarter, hidden), bf),
+                pltpu.VMEM((2, 2 * cap, hidden), bf),
+                pltpu.VMEM((2, 2 * cap, hidden), bf),
+                pltpu.VMEM((2, cap, 128), f32),
+                pltpu.VMEM((2, 2, cap, hidden), bf),
                 pltpu.VMEM((2, n_ing * cap, hidden), bf),
                 pltpu.VMEM((2, experts, tokens), i32),
                 pltpu.VMEM((2, experts, tokens), f32),
                 pltpu.VMEM((2, tokens, 128), i32),
-                dma((64,)), dma((60,)), dma((16,)), dma((16,)), dma((2,)), dma((2,)), dma(()), dma((2,)), dma((2,)),
+                dma((64,)), dma((60,)), dma((16,)), dma((16,)), dma((8,)), dma((2,)), dma((2,)), dma((2,)), dma((2,)), dma((2,)), dma((2,)),
             ],
             compiler_params=pltpu.CompilerParams(collective_id=0, has_side_effects=True, vmem_limit_bytes=67043328),
         )(x_first, x_second, ids, gates, wown)

time: 409 us -> 331 us (0.81)
  Pallas kernels: 395 us -> 317 us
    pallas_call x1, Pallas kernels: 395 us -> 317 us  [body(): pl.pallas_call(functools.partial(kernel, cap), out_shape=(y_shape, y_shap...]
where the time goes in v2:
time: 331 us; the launch traced here: 330 us
  Pallas kernels  317 us (96%)
  local copies, waits for them, and re-layouts  7.7 us (2%)
  other arithmetic  5.08 us (2%)
    pallas_call x1, Pallas kernels, body(): pl.pallas_call(functools.partial(kernel, cap), out_shape=(y_shape, y_shap...  317 us

profile of v2, /device:TPU:97, one launch (start us, length us, event | category | flops | bytes accessed | tf_op | source)
XLA Modules:
  0.0 330.2 jit_solution(9439494567113758347)
XLA Ops:
  0.6 0.0 copy-start.1
  0.6 0.0 copy-start.2
  0.7 1.6 pad_add_fusion.ids_ref
  2.3 1.5 pad_maximum_fusion.1.gates_ref
  3.7 1.8 reshape_squeeze.3
  5.6 0.2 copy.11
  5.8 0.0 copy-done.1
  5.8 0.0 copy-done.2
  5.8 2.0 pad_maximum_fusion.wown
  7.8 316.7 %shard_map.104 = (bf16[1536,1024]{1,0:T(8,128)(2,1)}, bf16[1536,1024]{1,0:T(8,128)(2,1)}, bf16[32,3,4,256,512]{4,3,2,1,0:T(8,128)(2,1)}, bf16[8,2,1536,1024]{3,2,1,0:T(8,128)(2,1)}, bf16[32,768,1024]{2,1,0:T(8,128)(2,1)}) custom-call(bf16[1536,1024]{1,0:T(8,128)(2,1)} %x_first.1, bf16[1536,1024]{1,0:T(8,128)(2,1)} %x_second.1, ...), custom_call_target="tpu_custom_call" | custom-call | tf_op jit(solution)/shard_map/pallas_call | solution.py:381
  324.5 0.0 copy-start
  324.5 4.0 %copy.14 = bf16[1536,1024]{1,0:T(8,128)(2,1)} copy(bf16[1536,1024]{1,0:T(8,128)(2,1)} %get-tuple-element.8) | data formatting | bytes 6291456
  328.6 0.0 copy-done
  328.6 1.7 copy.15
Async XLA Ops:
  0.6 5.1 %copy-start.1 = (bf16[1,1024,512]{2,1,0:T(8,128)(2,1)S(1)}, bf16[1,1024,512]{2,1,0:T(8,128)(2,1)}, u32[]{:S(2)}) copy-start(bf16[1,1024,512]{2,1,0:T(8,128)(2,1)} %param.16) | copy-start | bytes 3145732
  0.6 5.1 %copy-start.2 = (bf16[1,1024,512]{2,1,0:T(8,128)(2,1)S(1)}, bf16[1,1024,512]{2,1,0:T(8,128)(2,1)}, u32[]{:S(2)}) copy-start(bf16[1,1024,512]{2,1,0:T(8,128)(2,1)} %param.15) | copy-start | bytes 3145732
  324.5 4.0 %copy-start = (bf16[1536,1024]{1,0:T(8,128)(2,1)S(1)}, bf16[1536,1024]{1,0:T(8,128)(2,1)}, u32[]{:S(2)}) copy-start(bf16[1536,1024]{1,0:T(8,128)(2,1)} %get-tuple-element.9) | copy-start | bytes 9437188

commit v3 on v2

--- a/solution.py
+++ b/solution.py
@@ -8,12 +8,11 @@
 from jax.sharding import PartitionSpec as P
 
 MESH = pl.DeviceIdType.MESH
-AHEAD = 20
+AHEAD = 24
 RING = 4
 ORDER = [(0, 0), (0, 1), (0, 3), (1, 0), (3, 0), (0, 2), (1, 1), (1, 3), (1, 2), (3, 1), (3, 3), (3, 2), (2, 0), (2, 1), (2, 3), (2, 2)]
 GROUP_DX = [0, 0, 1, 1, 3, 3, 2, 2]
-UNIT_STEP = {1: (4, 0), 2: (11, 0), 3: (18, 0), 4: (21, 0), 5: (25, 0), 6: (28, 0), 7: (31, 0), 8: (31, 2), 9: (33, 0), 10: (35, 0),
-             11: (37, 2), 12: (39, 0), 13: (43, 1), 14: (43, 2), 15: (47, 0)}
+UNIT_STEP = {1: (5, 0), 2: (11, 0), 3: (18, 0), 4: (25, 0), 5: (28, 0), 6: (31, 0), 7: (35, 1), 8: (35, 2), 9: (39, 0), 10: (39, 0), 11: (41, 1), 12: (43, 0), 13: (47, 1), 14: (47, 2), 15: (52, 0)}
 
 
 def link_sends():
@@ -72,7 +71,7 @@
     return out
 
 
-def kernel(cap, x_first, x_second, ids_ref, gates_ref, wown, y_first, y_second, wall, zh, xh,
+def kernel(cap, x_first, x_second, ids_first, ids_second, gates_first, gates_second, w_one, w_three, w_two, y_first, y_second, wall, zh, xh,
            xv, yacc, w13, w2v, xs, xg, gb, zst, zc, slotrow, gaterow, slotcol,
            recv_sem, send_sem, d2d_recv, d2d_send, w_sem, x_sem, xo_sem, xi_sem, z_sem, zl_sem, y_sem):
     grp, y = lax.axis_index('grp'), lax.axis_index('ing')
@@ -80,7 +79,8 @@
     tokens = xv.shape[1]
     experts = slotrow.shape[1]
     per_group = RING
-    width = wown.shape[3]
+    width = wall.shape[4]
+    quarter = wall.shape[3]
     plan, units = make_plan()
     npos = RING * RING
 
@@ -98,21 +98,32 @@
         pl.semaphore_signal(barrier, inc=1, device_id=dev, device_id_type=MESH)
     pl.semaphore_wait(barrier, 5)
 
-    def quarter_copy(link, slot, item, target):
+    def own_piece(part, k):
+        if part < 2:
+            return (w_one, w_three)[part].at[0, pl.ds(k * quarter, quarter), :]
+        return w_two.at[0, pl.ds((k % 2) * quarter, quarter), pl.ds((k // 2) * width, width)]
+
+    def quarter_copies(link, slot, item, target):
         dx, dy, k = item
-        e = expert(dx, dy, c)
-        src = wown.at[:, k] if (dx, dy) == (0, 0) else wall.at[e, :, k]
-        return pltpu.make_async_remote_copy(
-            src_ref=src, dst_ref=wall.at[e, :, k], send_sem=send_sem.at[link * units + slot],
+        dst = wall.at[expert(dx, dy, c), :, k]
+        own = (dx, dy) == (0, 0)
+        pairs = [(own_piece(part, k), dst.at[part]) for part in range(3)] if own else [(dst, dst)]
+        return [pltpu.make_async_remote_copy(
+            src_ref=src, dst_ref=to, send_sem=send_sem.at[link * units + slot],
             recv_sem=recv_sem.at[(target[0] * RING + target[1]) * 4 + k], device_id=neighbour(link), device_id_type=MESH)
-
-    def d2d_copy(pos):
+            for src, to in pairs]
+
+    def d2d_copies(pos):
         j = ORDER.index(pos)
-        e = expert(*pos, c)
-        src = wown if j == 0 else wall.at[e]
-        return pltpu.make_async_remote_copy(
-            src_ref=src, dst_ref=wall.at[e], send_sem=d2d_send.at[j], recv_sem=d2d_recv.at[j],
-            device_id=partner, device_id_type=MESH)
+        dst = wall.at[expert(*pos, c)]
+        pairs = [(own_piece(part, k), dst.at[part, k]) for part in range(3) for k in range(4)] if j == 0 else [(dst, dst)]
+        return [pltpu.make_async_remote_copy(
+            src_ref=src, dst_ref=to, send_sem=d2d_send.at[j], recv_sem=d2d_recv.at[j],
+            device_id=partner, device_id_type=MESH) for src, to in pairs]
+
+    def sent(ref, sem):
+        pltpu.make_async_remote_copy(
+            src_ref=ref, dst_ref=ref, send_sem=sem, recv_sem=recv_sem.at[0], device_id=partner, device_id_type=MESH).wait_send()
 
     def act(unit):
         arrivals, issued, complete = plan[unit]
@@ -122,9 +133,11 @@
                 src_ref=ref, dst_ref=ref, send_sem=send_sem.at[0], recv_sem=recv_sem.at[(dx * RING + dy) * 4 + k],
                 device_id=partner, device_id_type=MESH).wait_recv()
         for link, slot, item, target in issued:
-            quarter_copy(link, slot, item, target).start()
+            for copy in quarter_copies(link, slot, item, target):
+                copy.start()
         for pos in complete:
-            d2d_copy(pos).start()
+            for copy in d2d_copies(pos):
+                copy.start()
 
     act(0)
     x_copies = [pltpu.make_async_copy(src, xv.at[m], x_sem.at[m]) for m, src in enumerate((x_first, x_second))]
@@ -137,8 +150,10 @@
         for half in range(2):
             yield pltpu.make_async_copy(src.at[2, pl.ds(2 * half, 2)], w2v.at[par, :, :, pl.ds(half * width, width)], w_sem.at[par * 4 + 2 + half])
 
-    for copy in weight_copies(wown, 0):
-        copy.start()
+    for k in range(4):
+        for part in range(2):
+            pltpu.make_async_copy(own_piece(part, k), w13.at[0, k, :, pl.ds(part * width, width)], w_sem.at[part]).start()
+        pltpu.make_async_copy(own_piece(2, k), w2v.at[0, k % 2, :, pl.ds((k // 2) * width, width)], w_sem.at[2 + k // 2]).start()
 
     lane_block = 128
     upper = (lax.broadcasted_iota(jnp.int32, (lane_block, lane_block), 0)
@@ -150,12 +165,12 @@
             cols = pl.ds(b * lane_block, lane_block)
             mem = jnp.zeros((experts, lane_block), jnp.float32)
             gat = jnp.zeros((experts, lane_block), jnp.float32)
-            for k in range(ids_ref.shape[1]):
-                hit = ids_ref[m, k:k + 1, cols] == e_iota
+            for k in range(ids_first.shape[0]):
+                hit = (ids_first, ids_second)[m][k:k + 1, cols] == e_iota
                 mem = jnp.where(hit, 1.0, mem)
-                gat = jnp.where(hit, gates_ref[m, k:k + 1, cols], gat)
+                gat = jnp.where(hit, (gates_first, gates_second)[m][k:k + 1, cols], gat)
             total = jnp.dot(mem.astype(jnp.bfloat16), upper, preferred_element_type=jnp.float32) + carry
-            carry = total[:, lane_block - 1:]
+            carry = carry + jnp.sum(mem, axis=1, keepdims=True)
             slot = jnp.where(mem > 0.0, total - 1.0, -1.0)
             slotrow[m, :, cols] = slot.astype(jnp.int32)
             gaterow[m, :, cols] = gat
@@ -208,7 +223,7 @@
             zst[par, m] = (out[m * cap:(m + 1) * cap] * gate).astype(jnp.bfloat16)
 
     def ready(s):
-        for copy in weight_copies(wown, s % 2):
+        for copy in weight_copies(wall.at[0], s % 2):
             copy.wait()
         row_in(s).wait()
 
@@ -227,7 +242,7 @@
                 copy.start()
         row_in(s).start()
 
-    def combine(base, groups, finish=None):
+    def combine(base, groups, step, near_end=None, finish=None):
         items = 2 * groups
 
         def load(i):
@@ -242,9 +257,18 @@
             g, copy = load(i)
             copy.wait()
 
+            @pl.when(i == 0)
+            def _():
+                z_copy(step).wait()
+
             @pl.when(i + 1 < items)
             def _():
                 load(i + 1)[1].start()
+
+            if near_end is not None:
+                @pl.when(i == items - 1)
+                def _():
+                    near_end()
 
             m = i // groups
             table = slotcol[m]
@@ -323,14 +347,15 @@
         @pl.when(late)
         def _():
             z_copy(s - 1).wait()
-            z_copy(s).wait()
             acts(1)
-            combine(jnp.where(s == last[0], 0, jnp.where(s == last[1], 2, 4)), 2)
-            acts(2)
-            fetch(s + 1)
+
+            def near_end():
+                acts(2)
+                fetch(s + 1)
+
+            combine(jnp.where(s == last[0], 0, jnp.where(s == last[1], 2, 4)), 2, s, near_end)
 
     z_copy(steps - 2).wait()
-    z_copy(steps - 1).wait()
 
     def finish(m):
         @pl.loop(0, tokens // 128)
@@ -342,16 +367,16 @@
             def _():
                 pltpu.make_async_copy(xv.at[n], dst, y_sem.at[n]).start()
 
-    combine(6, 2, finish)
+    combine(6, 2, steps - 1, None, finish)
     for m, dst in enumerate((y_first, y_second)):
         pltpu.make_async_copy(xv.at[m], dst, y_sem.at[m]).wait()
 
     for unit in range(units + 1):
         _, issued, complete = plan[unit]
         for link, slot, item, target in issued:
-            quarter_copy(link, slot, item, target).wait_send()
+            sent(wall.at[expert(item[0], item[1], c), :, item[2]], send_sem.at[link * units + slot])
         for pos in complete:
-            d2d_copy(pos).wait_send()
+            sent(wall.at[expert(*pos, c)], d2d_send.at[ORDER.index(pos)])
 
 
 def solution(mesh):
@@ -368,11 +393,8 @@
         limit_m = min(top_k, n_grp // 2)
         cap = limit_m * (-(-(tokens * (top_k // limit_m)) // experts))
         inner = w_one.shape[2]
-        ids = jnp.stack([ids_first.T, ids_second.T])
-        gates = jnp.stack([gates_first.T, gates_second.T])
         quarter = hidden // 4
-        w2 = w_two[0].reshape(2, inner // 2, 2, hidden // 2).transpose(2, 0, 1, 3).reshape(4, inner // 2, hidden // 2)
-        wown = jnp.stack([w_one[0].reshape(4, quarter, inner), w_three[0].reshape(4, quarter, inner), w2])
+        wall_shape = (experts, 3, 4, quarter, inner)
         bf, f32, i32 = jnp.bfloat16, jnp.float32, jnp.int32
         hbm = pl.BlockSpec(memory_space=pl.ANY)
         vmem = pl.BlockSpec(memory_space=pltpu.VMEM)
@@ -381,10 +403,10 @@
         outs = pl.pallas_call(
             functools.partial(kernel, cap),
             out_shape=(y_shape, y_shape,
-                       jax.ShapeDtypeStruct((experts,) + wown.shape, bf),
+                       jax.ShapeDtypeStruct(wall_shape, bf),
                        jax.ShapeDtypeStruct((n_grp, 2, n_ing * cap, hidden), bf),
                        jax.ShapeDtypeStruct((experts, 2 * cap, hidden), bf)),
-            in_specs=[hbm, hbm, vmem, vmem, hbm],
+            in_specs=[hbm] * 2 + [vmem] * 4 + [hbm] * 3,
             out_specs=(hbm,) * 5,
             scratch_shapes=[
                 pltpu.VMEM((2, tokens, hidden), bf),
@@ -402,7 +424,7 @@
                 dma((64,)), dma((60,)), dma((16,)), dma((16,)), dma((8,)), dma((2,)), dma((2,)), dma((2,)), dma((2,)), dma((2,)), dma((2,)),
             ],
             compiler_params=pltpu.CompilerParams(collective_id=0, has_side_effects=True, vmem_limit_bytes=67043328),
-        )(x_first, x_second, ids, gates, wown)
+        )(x_first, x_second, ids_first.T, ids_second.T, gates_first.T, gates_second.T, w_one, w_three, w_two)
         return outs[0], outs[1]
 
     return jax.shard_map(body, mesh=mesh, in_specs=(tok_spec,) * 6 + (w_spec,) * 3, out_specs=(tok_spec, tok_spec), check_vma=False)

time: 331 us -> 320 us (0.967)
  other arithmetic: 5.08 us -> 0 us
  Pallas kernels: 317 us -> 313 us
    another operation x3 -> x0, other arithmetic: 5.08 us -> none  [the longest x1 2 us: body(): jnp.stack([w_one[0].reshape(4, quarter, inner), w_three[0].reshape(4, qua...]
    pallas_call x1, Pallas kernels: 317 us -> 313 us  [body(): pl.pallas_call(functools.partial(kernel, cap), out_shape=(y_shape, y_shap...]
where the time goes in v3:
time: 320 us
  Pallas kernels  313 us (98%)
  local copies, waits for them, and re-layouts  5.69 us (2%)
    pallas_call x1, Pallas kernels, body(): pl.pallas_call(functools.partial(kernel, cap), out_shape=(y_shape, y_shap...  313 us

profile of v3, /device:TPU:97, one launch (start us, length us, event | category | flops | bytes accessed | tf_op | source)
XLA Modules:
  0.0 319.6 jit_solution(14988970011469086863)
XLA Ops:
  0.6 313.3 %shard_map.104 = (bf16[1536,1024]{1,0:T(8,128)(2,1)}, bf16[1536,1024]{1,0:T(8,128)(2,1)}, bf16[32,3,4,256,512]{4,3,2,1,0:T(8,128)(2,1)}, bf16[8,2,1536,1024]{3,2,1,0:T(8,128)(2,1)}, bf16[32,768,1024]{2,1,0:T(8,128)(2,1)}) custom-call(bf16[1536,1024]{1,0:T(8,128)(2,1)} %x_first.1, bf16[1536,1024]{1,0:T(8,128)(2,1)} %x_second.1, s32[8,1536]{1,0:T(8,128)} %bitcast.4, ...), custom_call_target="tpu_custom_call" | custom-call | tf_op jit(solution)/shard_map/pallas_call | solution.py:403
  313.9 0.0 copy-start
  313.9 4.0 %copy.13 = bf16[1536,1024]{1,0:T(8,128)(2,1)} copy(bf16[1536,1024]{1,0:T(8,128)(2,1)} %get-tuple-element.8) | data formatting | bytes 6291456
  317.9 0.0 copy-done
  317.9 1.7 copy.14
Async XLA Ops:
  313.9 4.0 %copy-start = (bf16[1536,1024]{1,0:T(8,128)(2,1)S(1)}, bf16[1536,1024]{1,0:T(8,128)(2,1)}, u32[]{:S(2)}) copy-start(bf16[1536,1024]{1,0:T(8,128)(2,1)} %get-tuple-element.9) | copy-start | bytes 9437188

commit v4 on v3

--- a/solution.py
+++ b/solution.py
@@ -113,10 +113,10 @@
             recv_sem=recv_sem.at[(target[0] * RING + target[1]) * 4 + k], device_id=neighbour(link), device_id_type=MESH)
             for src, to in pairs]
 
-    def d2d_copies(pos):
-        j = ORDER.index(pos)
-        dst = wall.at[expert(*pos, c)]
-        pairs = [(own_piece(part, k), dst.at[part, k]) for part in range(3) for k in range(4)] if j == 0 else [(dst, dst)]
+    def d2d_copies(dx, dy, k):
+        j = ORDER.index((dx, dy))
+        dst = wall.at[expert(dx, dy, c), :, k]
+        pairs = [(own_piece(part, k), dst.at[part]) for part in range(3)] if j == 0 else [(dst, dst)]
         return [pltpu.make_async_remote_copy(
             src_ref=src, dst_ref=to, send_sem=d2d_send.at[j], recv_sem=d2d_recv.at[j],
             device_id=partner, device_id_type=MESH) for src, to in pairs]
@@ -126,7 +126,7 @@
             src_ref=ref, dst_ref=ref, send_sem=sem, recv_sem=recv_sem.at[0], device_id=partner, device_id_type=MESH).wait_send()
 
     def act(unit):
-        arrivals, issued, complete = plan[unit]
+        arrivals, issued, _ = plan[unit]
         for dx, dy, k in arrivals:
             ref = wall.at[expert(dx, dy, c), :, k]
             pltpu.make_async_remote_copy(
@@ -135,8 +135,8 @@
         for link, slot, item, target in issued:
             for copy in quarter_copies(link, slot, item, target):
                 copy.start()
-        for pos in complete:
-            for copy in d2d_copies(pos):
+        for dx, dy, k in arrivals or [(0, 0, k) for k in range(4)]:
+            for copy in d2d_copies(dx, dy, k):
                 copy.start()
 
     act(0)
@@ -175,7 +175,7 @@
             slotrow[m, :, cols] = slot.astype(jnp.int32)
             gaterow[m, :, cols] = gat
             full = jnp.concatenate([slot, jnp.full((lane_block - experts, lane_block), -1.0, jnp.float32)], axis=0)
-            slotcol[m, cols, :] = full.T.astype(jnp.int32)
+            slotcol[m, cols, :] = full.T
 
     gb[...] = jnp.zeros_like(gb)
     for m in range(2):
@@ -273,10 +273,10 @@
             m = i // groups
             table = slotcol[m]
             lane = lax.broadcasted_iota(jnp.int32, table.shape, 1)
-            lane_cap = lax.broadcasted_iota(jnp.int32, (tokens, cap), 1)
+            lane_cap = lax.broadcasted_iota(jnp.int32, (tokens, cap), 1).astype(jnp.float32)
             parts = []
             for q in range(per_group):
-                col = jnp.sum(jnp.where(lane == g * per_group + q, table, 0), axis=1, keepdims=True)
+                col = jnp.sum(jnp.where(lane == g * per_group + q, table, 0.0), axis=1, keepdims=True)
                 parts.append((col == lane_cap).astype(jnp.bfloat16))
             sel = jnp.concatenate(parts, axis=1)
             part = jnp.dot(sel, zc[i % 2], preferred_element_type=jnp.float32)
@@ -420,7 +420,7 @@
                 pltpu.VMEM((2, n_ing * cap, hidden), bf),
                 pltpu.VMEM((2, experts, tokens), i32),
                 pltpu.VMEM((2, experts, tokens), f32),
-                pltpu.VMEM((2, tokens, 128), i32),
+                pltpu.VMEM((2, tokens, 128), f32),
                 dma((64,)), dma((60,)), dma((16,)), dma((16,)), dma((8,)), dma((2,)), dma((2,)), dma((2,)), dma((2,)), dma((2,)), dma((2,)),
             ],
             compiler_params=pltpu.CompilerParams(collective_id=0, has_side_effects=True, vmem_limit_bytes=67043328),

time: 320 us -> 317 us (level)
  no operation moved by 1% of the time
where the time goes in v4:
time: 317 us; the launch traced here: 316 us
  Pallas kernels  310 us (98%)
  local copies, waits for them, and re-layouts  5.69 us (2%)
    pallas_call x1, Pallas kernels, body(): pl.pallas_call(functools.partial(kernel, cap), out_shape=(y_shape, y_shap...  310 us

profile of v4, /device:TPU:97, one launch (start us, length us, event | category | flops | bytes accessed | tf_op | source)
XLA Modules:
  0.0 316.5 jit_solution(6829607792139382452)
XLA Ops:
  0.6 310.1 %shard_map.104 = (bf16[1536,1024]{1,0:T(8,128)(2,1)}, bf16[1536,1024]{1,0:T(8,128)(2,1)}, bf16[32,3,4,256,512]{4,3,2,1,0:T(8,128)(2,1)}, bf16[8,2,1536,1024]{3,2,1,0:T(8,128)(2,1)}, bf16[32,768,1024]{2,1,0:T(8,128)(2,1)}) custom-call(bf16[1536,1024]{1,0:T(8,128)(2,1)} %x_first.1, bf16[1536,1024]{1,0:T(8,128)(2,1)} %x_second.1, s32[8,1536]{1,0:T(8,128)} %bitcast.4, ...), custom_call_target="tpu_custom_call" | custom-call | tf_op jit(solution)/shard_map/pallas_call | solution.py:403
  310.8 0.0 copy-start
  310.8 4.0 %copy.13 = bf16[1536,1024]{1,0:T(8,128)(2,1)} copy(bf16[1536,1024]{1,0:T(8,128)(2,1)} %get-tuple-element.8) | data formatting | bytes 6291456
  314.8 0.0 copy-done
  314.8 1.7 copy.14
Async XLA Ops:
  310.8 4.0 %copy-start = (bf16[1536,1024]{1,0:T(8,128)(2,1)S(1)}, bf16[1536,1024]{1,0:T(8,128)(2,1)}, u32[]{:S(2)}) copy-start(bf16[1536,1024]{1,0:T(8,128)(2,1)} %get-tuple-element.9) | copy-start | bytes 9437188
